TPU v7x, 64 devices: a 2x2x8 block of a 4x4x8 slice. The times are simulated.
64 devices in a mesh: rep: 8 (over x, y, core), dp: 8 (over z).
Axes of the slice: x: 2, y: 2, z: 8, core: 2. Of those that a mesh axis runs over, the one named last changes fastest.
The devices are a block of a 4x4x8 slice.
Arguments:
- a: bfloat16 [64, 4, 8192, 512], P(('rep', 'dp')), parts along dimension 0
- g: bfloat16 [64, 4, 8192, 1280], P(('rep', 'dp')), parts along dimension 0
Outputs:
- output: bfloat16 [32, 512, 1280], P('rep'), parts along dimension 0
There are 8 independent parts. A program takes and returns all parts, laid end to end along the dimension named above; each array names one.
All inputs are finite; a program needn't handle non-finite values.
Results may differ from a plain program's by a relative error of at most 0.012.
Values are sent between devices in bfloat16 or wider.
A program may use at most 768 MiB of HBM per device.

v0:
```python
import jax
import jax.numpy as jnp


def solution(mesh):
    groups = mesh.shape["rep"]

    def step(a, g):
        a, g = (t.reshape(groups, -1, *t.shape[1:]) for t in (a, g))
        sums = jnp.einsum("rsntd,rsntf->rndf", a, g, preferred_element_type=jnp.float32)
        return sums.astype(jnp.bfloat16).reshape(-1, *sums.shape[2:])

    return step
```

profile of v0, /device:TPU:22, one launch (start us, length us, event | category | flops | bytes accessed | tf_op | source)
XLA Modules:
  0.0 269.8 jit_solution(17330229871913991300)
XLA Ops:
  0.0 55.4 %fusion.3 = f32[1,4,512,1280]{3,2,1,0:T(8,128)} fusion(bf16[1,4,8192,1280]{3,2,1,0:T(8,128)(2,1)} %param.1, bf16[1,4,8192,512]{3,2,1,0:T(8,128)(2,1)} %param), kind=kOutput, calls=%fused_computation.3 | convolution fusion | flops 42949672960 | bytes 127926272 | tf_op jit(solution)/rsntd,rsntf->rndf/dot_general | solution.py:10
  55.4 214.4 %all-reduce.2 = bf16[1,4,512,1280]{3,2,1,0:T(8,128)(2,1)} all-reduce(f32[1,4,512,1280]{3,2,1,0:T(8,128)} %fusion.3), channel_id=1, replica_groups=[8,8]<=[64], use_global_device_ids=true, to_apply=%add.clone | all-reduce | flops 2621440 | bytes 15728640 | tf_op jit(solution)/rsntd,rsntf->rndf/dot_general | solution.py:10
where the time goes:
time: 270 us
  blocking collectives  214 us (79%)
  matrix products  55.4 us (21%)
    dot_general x1, blocking collectives, step(): jnp.einsum('rsntd,rsntf->rndf', a, g, preferred_element_type=jnp.float32)  214 us
    dot_general x1, matrix products, step(): jnp.einsum('rsntd,rsntf->rndf', a, g, preferred_element_type=jnp.float32)  55.4 us

commit v1 on v0

v1 whole, which is shorter than its diff:
```python
import functools

import jax
import jax.numpy as jnp
from jax import lax
from jax.experimental import pallas as pl
from jax.experimental.pallas import tpu as pltpu
from jax.sharding import PartitionSpec as P

MESH = pl.DeviceIdType.MESH
COLS = 256
PIECES = 8
DOTS = 4
SLOTS = 6
GBUF = 3


def kernel(shape, a_hbm, g_hbm, out, a_raw, a_t, g_buf, own, first, runs, a_sem, g_sem, send_sem, recv_sem):
    n, matrices, tokens, d, ff = shape
    per = ff // COLS
    chunks = matrices * per
    rows = d // n
    half = rows // 2
    far = n // 2
    me = lax.axis_index("dp")
    right, left = lax.rem(me + 1, n), lax.rem(me + n - 1, n)
    piece = tokens // PIECES
    depth = tokens // DOTS
    low, high = pl.ds(0, half), pl.ds(half, half)

    def owner(offset):
        return lax.rem(me + offset + n, n)

    def rows_of(who, lo=0, size=rows):
        return pl.ds(pl.multiple_of(who * rows + lo, half), size)

    def place(c, who, lo=0, size=rows):
        return out.at[c // per, rows_of(who, lo, size), pl.ds(pl.multiple_of(lax.rem(c, per) * COLS, COLS), COLS)]

    def load_a(m, k):
        r = pl.ds(k * piece, piece)
        return pltpu.make_async_copy(a_hbm.at[0, m, r], a_raw.at[r], a_sem.at[k])

    def load_g(c, k):
        r = pl.ds(k * piece, piece)
        col = pl.ds(pl.multiple_of(lax.rem(c, per) * COLS, COLS), COLS)
        return pltpu.make_async_copy(g_hbm.at[0, c // per, r, col], g_buf.at[lax.rem(c, GBUF), r], g_sem.at[lax.rem(c, GBUF), k])

    def send(way, stage, c, src, dst):
        return pltpu.make_async_remote_copy(
            src_ref=src, dst_ref=dst, send_sem=send_sem.at[way, stage, c], recv_sem=recv_sem.at[way, stage, c],
            device_id={"dp": right if way == 0 else left}, device_id_type=MESH)

    def hop(way, s, c):
        if s == 0:
            part = low if way == 0 else high
            return send(way, 0, c, first.at[c, part], runs.at[way, 0, c, part])
        return send(way, s, c, runs.at[way, s - 1, c], runs.at[way, s, c])

    def originate(c):
        who = owner(far)
        first[c] = own[lax.rem(c, SLOTS), rows_of(who)].astype(jnp.bfloat16)
        for way in (0, 1):
            hop(way, 0, c).start()

    def pass_on(s, c):
        for way in (0, 1):
            who = owner(far - s if way == 0 else s - far)
            hop(way, s - 1, c).wait_recv()
            mine = own.at[lax.rem(c, SLOTS), rows_of(who)]
            if s == 1:
                add, plain = (low, high) if way == 0 else (high, low)
                runs[way, 0, c, add] = (runs[way, 0, c, add].astype(jnp.float32) + mine[add]).astype(jnp.bfloat16)
                runs[way, 0, c, plain] = mine[plain].astype(jnp.bfloat16)
            else:
                runs[way, s - 1, c] = (runs[way, s - 1, c].astype(jnp.float32) + mine[...]).astype(jnp.bfloat16)
            hop(way, s, c).start()

    def spread(way, h, c, who):
        if h == far:
            ref = place(c, who, 0 if way == 0 else half, half)
        else:
            ref = place(c, who)
        return send(way, far + h - 1, c, ref, ref)

    def spread_out(way, h, c):
        return spread(way, h, c, owner(1 - h if way == 0 else h - 1))

    def spread_in(way, h, c):
        return spread(way, h, c, owner(-h if way == 0 else h))

    def finish(c):
        for way in (0, 1):
            hop(way, far - 1, c).wait_recv()
        total = own[lax.rem(c, SLOTS), rows_of(me)]
        total = total + runs[0, far - 1, c].astype(jnp.float32) + runs[1, far - 1, c].astype(jnp.float32)
        place(c, me)[...] = total.astype(jnp.bfloat16)
        for way in (0, 1):
            spread_out(way, 1, c).start()

    def forward(h, c):
        for way in (0, 1):
            spread_in(way, h - 1, c).wait_recv()
            spread_out(way, h, c).start()

    def phase(t, p):
        if p < 3:
            c = t - 2 - p

            @pl.when((c >= 0) & (c < chunks))
            def _():
                pass_on(p + 1, c)
        else:
            @pl.when((t >= 5) & (t < chunks + 5))
            def _():
                finish(t - 5)

            @pl.when(t < chunks)
            def _():
                originate(t)

    def tick(t, m, fresh):
        slot = lax.rem(t, SLOTS)
        buf = lax.rem(t, GBUF)

        @pl.when(t + GBUF - 1 < chunks)
        def _():
            for k in range(PIECES):
                load_g(t + GBUF - 1, k).start()

        if not fresh:
            @pl.when((lax.rem(t, per) == 1) & (m + 1 < matrices))
            def _():
                for k in range(PIECES):
                    load_a(m + 1, k).start()

        for k in range(DOTS):
            for q in range(k * PIECES // DOTS, (k + 1) * PIECES // DOTS):
                if fresh:
                    load_a(m, q).wait()
                load_g(t, q).wait()
            r = pl.ds(k * depth, depth)
            if fresh:
                a_t[:, r] = a_raw[r, :].T
            part = jnp.dot(a_t[:, r], g_buf[buf, r], preferred_element_type=jnp.float32)
            if k == 0:
                own[slot] = part
            else:
                own[slot] += part
            phase(t, k)

    for k in range(PIECES):
        load_a(0, k).start()
        load_g(0, k).start()
    for k in range(PIECES):
        load_g(1, k).start()

    barrier = pltpu.get_barrier_semaphore()
    for other in (left, right):
        pl.semaphore_signal(barrier, inc=1, device_id={"dp": other}, device_id_type=MESH)
    pl.semaphore_wait(barrier, 2)

    @pl.loop(0, matrices)
    def _(m):
        tick(m * per, m, True)

        @pl.loop(1, per)
        def _(j):
            tick(m * per + j, m, False)

    early = 3 * 5

    @pl.loop(0, 5)
    def _(i):
        for p in range(4):
            phase(chunks + i, p)
            if p < 3:
                forward(2, 3 * i + p)

    @pl.loop(early, chunks)
    def _(c):
        forward(2, c)

    for h in range(3, far + 1):
        @pl.loop(0, chunks)
        def _(c):
            forward(h, c)

    @pl.loop(0, chunks)
    def _(c):
        for way in (0, 1):
            spread_in(way, far, c).wait_recv()

    @pl.loop(0, chunks)
    def _(c):
        for way in (0, 1):
            for s in range(far):
                hop(way, s, c).wait_send()
            for h in range(1, far + 1):
                spread_out(way, h, c).wait_send()


def solution(mesh):
    n = mesh.shape["dp"]

    def step(a, g):
        _, matrices, tokens, d = a.shape
        ff = g.shape[-1]
        chunks = matrices * (ff // COLS)
        rows = d // n
        far = n // 2
        bf16, f32 = jnp.bfloat16, jnp.float32
        return pl.pallas_call(
            functools.partial(kernel, (n, matrices, tokens, d, ff)),
            out_shape=jax.ShapeDtypeStruct((matrices, d, ff), bf16),
            in_specs=[pl.BlockSpec(memory_space=pl.ANY)] * 2,
            out_specs=pl.BlockSpec(memory_space=pltpu.VMEM),
            scratch_shapes=[
                pltpu.VMEM((tokens, d), bf16),
                pltpu.VMEM((d, tokens), bf16),
                pltpu.VMEM((GBUF, tokens, COLS), bf16),
                pltpu.VMEM((SLOTS, d, COLS), f32),
                pltpu.VMEM((chunks, rows, COLS), bf16),
                pltpu.VMEM((2, far, chunks, rows, COLS), bf16),
                pltpu.SemaphoreType.DMA((PIECES,)),
                pltpu.SemaphoreType.DMA((GBUF, PIECES)),
                pltpu.SemaphoreType.DMA((2, 2 * far, chunks)),
                pltpu.SemaphoreType.DMA((2, 2 * far, chunks)),
            ],
            compiler_params=pltpu.CompilerParams(
                collective_id=0, has_side_effects=True, vmem_limit_bytes=66_000_000
            ),
        )(a, g)

    return jax.shard_map(
        step, mesh=mesh, in_specs=(P(("rep", "dp")), P(("rep", "dp"))), out_specs=P("rep"), check_vma=False
    )
```

time: 270 us -> 176 us (0.65)
  blocking collectives: 214 us -> 0 us
  Pallas kernels: 0 us -> 170 us
  matrix products: 55.4 us -> 0 us
  local copies, waits for them, and re-layouts: 0 us -> 5.18 us
    dot_general x1 -> x0, blocking collectives: 214 us -> none  [step(): jnp.einsum('rsntd,rsntf->rndf', a, g, preferred_element_type=jnp.float32)]
    pallas_call x0 -> x1, Pallas kernels: none -> 170 us  [step(): pl.pallas_call(functools.partial(kernel, (n, matrices, tokens, d, ff)), o...]
    dot_general x1 -> x0, matrix products: 55.4 us -> none  [step(): jnp.einsum('rsntd,rsntf->rndf', a, g, preferred_element_type=jnp.float32)]
    unnamed x0 -> x1, local copies, waits for them, and re-layouts: none -> 5.18 us
where the time goes in v1:
time: 176 us; the launch traced here: 175 us
  Pallas kernels  170 us (97%)
  local copies, waits for them, and re-layouts  5.18 us (3%)
    pallas_call x1, Pallas kernels, step(): pl.pallas_call(functools.partial(kernel, (n, matrices, tokens, d, ff)), o...  170 us
    unnamed x1, local copies, waits for them, and re-layouts  5.18 us

profile of v1, /device:TPU:22, one launch (start us, length us, event | category | flops | bytes accessed | tf_op | source)
XLA Modules:
  0.0 175.3 jit_solution(12438187666780642283)
XLA Ops:
  0.0 170.1 %shard_map.28 = bf16[4,512,1280]{2,1,0:T(8,128)(2,1)} custom-call(bf16[1,4,8192,512]{3,2,1,0:T(8,128)(2,1)} %a_hbm.1, bf16[1,4,8192,1280]{3,2,1,0:T(8,128)(2,1)} %g_hbm.1), custom_call_target="tpu_custom_call" | custom-call | tf_op jit(solution)/shard_map/pallas_call | solution.py:213
  170.1 5.2 %copy.4 = bf16[4,512,1280]{2,1,0:T(8,128)(2,1)} copy(bf16[4,512,1280]{2,1,0:T(8,128)(2,1)} %shard_map.28) | data formatting | bytes 10485760

commit v2 on v1

--- a/solution.py
+++ b/solution.py
@@ -10,9 +10,18 @@
 MESH = pl.DeviceIdType.MESH
 COLS = 256
 PIECES = 8
-DOTS = 4
-SLOTS = 6
+DOTS = 2
+LAG = 5
+SLOTS = LAG + 1
 GBUF = 3
+
+
+def when(condition, then):
+    if isinstance(condition, bool):
+        if condition:
+            then()
+    else:
+        pl.when(condition)(then)
 
 
 def kernel(shape, a_hbm, g_hbm, out, a_raw, a_t, g_buf, own, first, runs, a_sem, g_sem, send_sem, recv_sem):
@@ -25,7 +34,6 @@
     me = lax.axis_index("dp")
     right, left = lax.rem(me + 1, n), lax.rem(me + n - 1, n)
     piece = tokens // PIECES
-    depth = tokens // DOTS
     low, high = pl.ds(0, half), pl.ds(half, half)
 
     def owner(offset):
@@ -77,10 +85,12 @@
             hop(way, s, c).start()
 
     def spread(way, h, c, who):
-        if h == far:
-            ref = place(c, who, 0 if way == 0 else half, half)
+        if h == 1:
+            ref = place(c, who)
+        elif h == far:
+            ref = out.at[c, rows_of(who, 0 if way == 0 else half, half)]
         else:
-            ref = place(c, who)
+            ref = out.at[c, rows_of(who)]
         return send(way, far + h - 1, c, ref, ref)
 
     def spread_out(way, h, c):
@@ -98,35 +108,37 @@
         for way in (0, 1):
             spread_out(way, 1, c).start()
 
-    def forward(h, c):
-        for way in (0, 1):
-            spread_in(way, h - 1, c).wait_recv()
-            spread_out(way, h, c).start()
+    def forward(h, m):
+        for way in (0, 1):
+            if h == 2:
+                for j in range(per):
+                    spread_in(way, 1, m * per + j).wait_recv()
+            else:
+                spread_in(way, h - 1, m).wait_recv()
+            spread_out(way, h, m).start()
 
     def phase(t, p):
-        if p < 3:
-            c = t - 2 - p
-
-            @pl.when((c >= 0) & (c < chunks))
-            def _():
-                pass_on(p + 1, c)
+        def hops(s, c):
+            when((c >= 0) & (c < chunks), lambda: pass_on(s, c))
+
+        if p == 0:
+            hops(2, t - 3)
+            hops(3, t - 4)
         else:
-            @pl.when((t >= 5) & (t < chunks + 5))
-            def _():
-                finish(t - 5)
-
-            @pl.when(t < chunks)
-            def _():
-                originate(t)
-
-    def tick(t, m, fresh):
+            when(t < chunks, lambda: originate(t))
+            hops(1, t - 1)
+            when((t >= LAG) & (t < chunks + LAG), lambda: finish(t - LAG))
+
+    def tick(t, m, fresh, dots=DOTS):
         slot = lax.rem(t, SLOTS)
         buf = lax.rem(t, GBUF)
 
-        @pl.when(t + GBUF - 1 < chunks)
-        def _():
+        def more():
             for k in range(PIECES):
                 load_g(t + GBUF - 1, k).start()
+
+        if dots == DOTS:
+            when(t + GBUF - 1 < chunks, more)
 
         if not fresh:
             @pl.when((lax.rem(t, per) == 1) & (m + 1 < matrices))
@@ -134,33 +146,47 @@
                 for k in range(PIECES):
                     load_a(m + 1, k).start()
 
-        for k in range(DOTS):
-            for q in range(k * PIECES // DOTS, (k + 1) * PIECES // DOTS):
+        depth = tokens // dots
+        for k in range(dots):
+            for q in range(k * PIECES // dots, (k + 1) * PIECES // dots):
                 if fresh:
                     load_a(m, q).wait()
                 load_g(t, q).wait()
+            if dots == PIECES and k >= 5:
+                for q in ((0, 1), (2, 3, 4), (5, 6, 7))[k - 5]:
+                    load_g(1, q).start()
             r = pl.ds(k * depth, depth)
             if fresh:
                 a_t[:, r] = a_raw[r, :].T
-            part = jnp.dot(a_t[:, r], g_buf[buf, r], preferred_element_type=jnp.float32)
-            if k == 0:
-                own[slot] = part
-            else:
-                own[slot] += part
-            phase(t, k)
+            for i in range(2):
+                rr = pl.ds(i * (d // 2), d // 2)
+                part = jnp.dot(a_t[rr, r], g_buf[buf, r], preferred_element_type=jnp.float32)
+                if k == 0:
+                    own[slot, rr] = part
+                else:
+                    own[slot, rr] += part
+            if dots == DOTS:
+                phase(t, k)
+
+    barrier = pltpu.get_barrier_semaphore()
+    for other in (left, right):
+        pl.semaphore_signal(barrier, inc=1, device_id={"dp": other}, device_id_type=MESH)
 
     for k in range(PIECES):
         load_a(0, k).start()
         load_g(0, k).start()
+
+    tick(0, 0, True, PIECES)
+    pl.semaphore_wait(barrier, 2)
+    originate(0)
     for k in range(PIECES):
-        load_g(1, k).start()
-
-    barrier = pltpu.get_barrier_semaphore()
-    for other in (left, right):
-        pl.semaphore_signal(barrier, inc=1, device_id={"dp": other}, device_id_type=MESH)
-    pl.semaphore_wait(barrier, 2)
-
-    @pl.loop(0, matrices)
+        load_g(2, k).start()
+
+    @pl.loop(1, per)
+    def _(t):
+        tick(t, 0, False)
+
+    @pl.loop(1, matrices)
     def _(m):
         tick(m * per, m, True)
 
@@ -168,36 +194,30 @@
         def _(j):
             tick(m * per + j, m, False)
 
-    early = 3 * 5
-
-    @pl.loop(0, 5)
-    def _(i):
-        for p in range(4):
+    for i in range(LAG):
+        for p in range(DOTS):
             phase(chunks + i, p)
-            if p < 3:
-                forward(2, 3 * i + p)
-
-    @pl.loop(early, chunks)
-    def _(c):
-        forward(2, c)
-
-    for h in range(3, far + 1):
-        @pl.loop(0, chunks)
-        def _(c):
-            forward(h, c)
+        if i in (0, 2):
+            forward(2, i // 2)
+
+    for h, m in ((2, 2), (3, 0), (2, 3), (3, 1), (4, 0), (3, 2), (4, 1), (3, 3), (4, 2), (4, 3)):
+        forward(h, m)
+
+    for m in range(matrices):
+        for way in (0, 1):
+            spread_in(way, far, m).wait_recv()
 
     @pl.loop(0, chunks)
     def _(c):
         for way in (0, 1):
-            spread_in(way, far, c).wait_recv()
-
-    @pl.loop(0, chunks)
-    def _(c):
-        for way in (0, 1):
             for s in range(far):
                 hop(way, s, c).wait_send()
-            for h in range(1, far + 1):
-                spread_out(way, h, c).wait_send()
+            spread_out(way, 1, c).wait_send()
+
+    for m in range(matrices):
+        for way in (0, 1):
+            for h in range(2, far + 1):
+                spread_out(way, h, m).wait_send()
 
 
 def solution(mesh):
@@ -212,7 +232,7 @@
         bf16, f32 = jnp.bfloat16, jnp.float32
         return pl.pallas_call(
             functools.partial(kernel, (n, matrices, tokens, d, ff)),
-            out_shape=jax.ShapeDtypeStruct((matrices, d, ff), bf16),
+            out_shape=pltpu.VMEM((matrices, d, ff), bf16),
             in_specs=[pl.BlockSpec(memory_space=pl.ANY)] * 2,
             out_specs=pl.BlockSpec(memory_space=pltpu.VMEM),
             scratch_shapes=[
@@ -228,7 +248,7 @@
                 pltpu.SemaphoreType.DMA((2, 2 * far, chunks)),
             ],
             compiler_params=pltpu.CompilerParams(
-                collective_id=0, has_side_effects=True, vmem_limit_bytes=66_000_000
+                collective_id=0, has_side_effects=True, vmem_limit_bytes=56_000_000
             ),
         )(a, g)
 

time: 176 us -> 130 us (0.74)
  Pallas kernels: 170 us -> 128 us
  local copies, waits for them, and re-layouts: 5.18 us -> 2.36 us
    pallas_call x1, Pallas kernels: 170 us -> 128 us  [step(): pl.pallas_call(functools.partial(kernel, (n, matrices, tokens, d, ff)), o...]
    unnamed x1, local copies, waits for them, and re-layouts: 5.18 us -> 2.36 us
where the time goes in v2:
time: 130 us
  Pallas kernels  128 us (98%)
  local copies, waits for them, and re-layouts  2.36 us (2%)
    pallas_call x1, Pallas kernels, step(): pl.pallas_call(functools.partial(kernel, (n, matrices, tokens, d, ff)), o...  128 us

profile of v2, /device:TPU:22, one launch (start us, length us, event | category | flops | bytes accessed | tf_op | source)
XLA Modules:
  0.0 130.1 jit_solution(9418932320314514642)
XLA Ops:
  0.0 127.8 %shard_map.28 = bf16[4,512,1280]{2,1,0:T(8,128)(2,1)S(1)} custom-call(bf16[1,4,8192,512]{3,2,1,0:T(8,128)(2,1)} %a_hbm.1, bf16[1,4,8192,1280]{3,2,1,0:T(8,128)(2,1)} %g_hbm.1), custom_call_target="tpu_custom_call" | custom-call | tf_op jit(solution)/shard_map/pallas_call | solution.py:233
  127.8 2.4 %copy.4 = bf16[4,512,1280]{2,1,0:T(8,128)(2,1)} copy(bf16[4,512,1280]{2,1,0:T(8,128)(2,1)S(1)} %shard_map.28) | data formatting | bytes 10485760

commit v3 on v2

--- a/solution.py
+++ b/solution.py
@@ -194,18 +194,14 @@
         def _(j):
             tick(m * per + j, m, False)
 
+    between = ((2, 0), (2, 1), (2, 2), (3, 0), (3, 1))
     for i in range(LAG):
         for p in range(DOTS):
             phase(chunks + i, p)
-        if i in (0, 2):
-            forward(2, i // 2)
-
-    for h, m in ((2, 2), (3, 0), (2, 3), (3, 1), (4, 0), (3, 2), (4, 1), (3, 3), (4, 2), (4, 3)):
-        forward(h, m)
-
-    for m in range(matrices):
-        for way in (0, 1):
-            spread_in(way, far, m).wait_recv()
+        forward(*between[i])
+
+    forward(2, 3)
+    forward(3, 2)
 
     @pl.loop(0, chunks)
     def _(c):
@@ -214,10 +210,18 @@
                 hop(way, s, c).wait_send()
             spread_out(way, 1, c).wait_send()
 
+    for h, m in ((3, 3), (4, 0), (4, 1), (4, 2), (4, 3)):
+        forward(h, m)
+
+    for h in range(2, far):
+        for m in range(matrices):
+            for way in (0, 1):
+                spread_out(way, h, m).wait_send()
+
     for m in range(matrices):
         for way in (0, 1):
-            for h in range(2, far + 1):
-                spread_out(way, h, m).wait_send()
+            spread_out(way, far, m).wait_send()
+            spread_in(way, far, m).wait_recv()
 
 
 def solution(mesh):

time: 130 us -> 128 us (0.985)
  Pallas kernels: 128 us -> 125 us
    pallas_call x1, Pallas kernels: 128 us -> 125 us  [step(): pl.pallas_call(functools.partial(kernel, (n, matrices, tokens, d, ff)), o...]
where the time goes in v3:
time: 128 us
  Pallas kernels  125 us (98%)
  local copies, waits for them, and re-layouts  2.36 us (2%)
    pallas_call x1, Pallas kernels, step(): pl.pallas_call(functools.partial(kernel, (n, matrices, tokens, d, ff)), o...  125 us

profile of v3, /device:TPU:22, one launch (start us, length us, event | category | flops | bytes accessed | tf_op | source)
XLA Modules:
  0.0 127.5 jit_solution(11358307907135702354)
XLA Ops:
  0.0 125.2 %shard_map.28 = bf16[4,512,1280]{2,1,0:T(8,128)(2,1)S(1)} custom-call(bf16[1,4,8192,512]{3,2,1,0:T(8,128)(2,1)} %a_hbm.1, bf16[1,4,8192,1280]{3,2,1,0:T(8,128)(2,1)} %g_hbm.1), custom_call_target="tpu_custom_call" | custom-call | tf_op jit(solution)/shard_map/pallas_call | solution.py:237
  125.2 2.4 %copy.4 = bf16[4,512,1280]{2,1,0:T(8,128)(2,1)} copy(bf16[4,512,1280]{2,1,0:T(8,128)(2,1)S(1)} %shard_map.28) | data formatting | bytes 10485760

commit v4 on v3

--- a/solution.py
+++ b/solution.py
@@ -11,7 +11,7 @@
 COLS = 256
 PIECES = 8
 DOTS = 2
-LAG = 5
+LAG = 6
 SLOTS = LAG + 1
 GBUF = 3
 
@@ -59,29 +59,35 @@
             src_ref=src, dst_ref=dst, send_sem=send_sem.at[way, stage, c], recv_sem=recv_sem.at[way, stage, c],
             device_id={"dp": right if way == 0 else left}, device_id_type=MESH)
 
+    def long_of(way):
+        return low if way == 0 else high
+
+    def short_of(way):
+        return high if way == 0 else low
+
     def hop(way, s, c):
-        if s == 0:
-            part = low if way == 0 else high
-            return send(way, 0, c, first.at[c, part], runs.at[way, 0, c, part])
-        return send(way, s, c, runs.at[way, s - 1, c], runs.at[way, s, c])
+        src = first.at[way, c] if s == 0 else runs.at[way, s - 1, c]
+        dst = runs.at[way, s, c]
+        if s == far - 1:
+            src, dst = src.at[long_of(way)], dst.at[long_of(way)]
+        return send(way, s, c, src, dst)
+
+    def mine(way, s, c, part):
+        hops = far - s if part is long_of(way) else far - 1 - s
+        return own[lax.rem(c, SLOTS), rows_of(owner(hops if way == 0 else -hops), part.start, half)]
 
     def originate(c):
-        who = owner(far)
-        first[c] = own[lax.rem(c, SLOTS), rows_of(who)].astype(jnp.bfloat16)
-        for way in (0, 1):
+        for way in (0, 1):
+            for part in (low, high):
+                first[way, c, part] = mine(way, 0, c, part).astype(jnp.bfloat16)
             hop(way, 0, c).start()
 
     def pass_on(s, c):
         for way in (0, 1):
-            who = owner(far - s if way == 0 else s - far)
             hop(way, s - 1, c).wait_recv()
-            mine = own.at[lax.rem(c, SLOTS), rows_of(who)]
-            if s == 1:
-                add, plain = (low, high) if way == 0 else (high, low)
-                runs[way, 0, c, add] = (runs[way, 0, c, add].astype(jnp.float32) + mine[add]).astype(jnp.bfloat16)
-                runs[way, 0, c, plain] = mine[plain].astype(jnp.bfloat16)
-            else:
-                runs[way, s - 1, c] = (runs[way, s - 1, c].astype(jnp.float32) + mine[...]).astype(jnp.bfloat16)
+            for part in (low, high) if s < far - 1 else (long_of(way),):
+                total = runs[way, s - 1, c, part].astype(jnp.float32) + mine(way, s, c, part)
+                runs[way, s - 1, c, part] = total.astype(jnp.bfloat16)
             hop(way, s, c).start()
 
     def spread(way, h, c, who):
@@ -102,9 +108,11 @@
     def finish(c):
         for way in (0, 1):
             hop(way, far - 1, c).wait_recv()
-        total = own[lax.rem(c, SLOTS), rows_of(me)]
-        total = total + runs[0, far - 1, c].astype(jnp.float32) + runs[1, far - 1, c].astype(jnp.float32)
-        place(c, me)[...] = total.astype(jnp.bfloat16)
+        for way in (0, 1):
+            part = long_of(way)
+            total = own[lax.rem(c, SLOTS), rows_of(me, part.start, half)]
+            total = total + runs[way, far - 1, c, part].astype(jnp.float32) + runs[1 - way, far - 2, c, part].astype(jnp.float32)
+            place(c, me, part.start, half)[...] = total.astype(jnp.bfloat16)
         for way in (0, 1):
             spread_out(way, 1, c).start()
 
@@ -122,11 +130,11 @@
             when((c >= 0) & (c < chunks), lambda: pass_on(s, c))
 
         if p == 0:
-            hops(2, t - 3)
-            hops(3, t - 4)
+            hops(1, t - 2)
+            hops(3, t - 5)
         else:
             when(t < chunks, lambda: originate(t))
-            hops(1, t - 1)
+            hops(2, t - 3)
             when((t >= LAG) & (t < chunks + LAG), lambda: finish(t - LAG))
 
     def tick(t, m, fresh, dots=DOTS):
@@ -198,7 +206,8 @@
     for i in range(LAG):
         for p in range(DOTS):
             phase(chunks + i, p)
-        forward(*between[i])
+        if i > 0:
+            forward(*between[i - 1])
 
     forward(2, 3)
     forward(3, 2)
@@ -244,7 +253,7 @@
                 pltpu.VMEM((d, tokens), bf16),
                 pltpu.VMEM((GBUF, tokens, COLS), bf16),
                 pltpu.VMEM((SLOTS, d, COLS), f32),
-                pltpu.VMEM((chunks, rows, COLS), bf16),
+                pltpu.VMEM((2, chunks, rows, COLS), bf16),
                 pltpu.VMEM((2, far, chunks, rows, COLS), bf16),
                 pltpu.SemaphoreType.DMA((PIECES,)),
                 pltpu.SemaphoreType.DMA((GBUF, PIECES)),

time: 128 us -> 127 us (level)
    pallas_call x1, Pallas kernels: 125 us -> 124 us  [step(): pl.pallas_call(functools.partial(kernel, (n, matrices, tokens, d, ff)), o...]
where the time goes in v4:
time: 127 us; the launch traced here: 126 us
  Pallas kernels  124 us (98%)
  local copies, waits for them, and re-layouts  2.36 us (2%)
    pallas_call x1, Pallas kernels, step(): pl.pallas_call(functools.partial(kernel, (n, matrices, tokens, d, ff)), o...  124 us

profile of v4, /device:TPU:22, one launch (start us, length us, event | category | flops | bytes accessed | tf_op | source)
XLA Modules:
  0.0 126.2 jit_solution(10102017242940176713)
XLA Ops:
  0.0 123.8 %shard_map.28 = bf16[4,512,1280]{2,1,0:T(8,128)(2,1)S(1)} custom-call(bf16[1,4,8192,512]{3,2,1,0:T(8,128)(2,1)} %a_hbm.1, bf16[1,4,8192,1280]{3,2,1,0:T(8,128)(2,1)} %g_hbm.1), custom_call_target="tpu_custom_call" | custom-call | tf_op jit(solution)/shard_map/pallas_call | solution.py:246
  123.8 2.4 %copy.4 = bf16[4,512,1280]{2,1,0:T(8,128)(2,1)} copy(bf16[4,512,1280]{2,1,0:T(8,128)(2,1)S(1)} %shard_map.28) | data formatting | bytes 10485760
